TPU v7x, 256 devices: a whole 4x4x8 slice. The times are simulated.
256 devices in a mesh: tok: 32 (over z_lo, x, core), blk: 8 (over y, z_hi).
Axes of the slice: x: 4, y: 4, z: 8 (z_hi: 2, z_lo: 4; z = z_hi * 4 + z_lo), core: 2. Of those that a mesh axis runs over, the one named last changes fastest.
Arguments:
- activations: bfloat16 [4096, 7168], P('tok', 'blk'), may hold values from -600 to 600
- signs: float32 [7168], P('blk'), may hold values from -1 to 1, as said below
Outputs:
- hessian: float32 [7168, 7168], P('tok', 'blk')
- incoherence: float32 [7168], P('blk')
- largest_ratio: float32 [], replicated
Inputs may be any that keep to these rules, and one draw needn't show every extreme that they name: `signs`: every entry is -1 or 1.
All inputs are finite; a program needn't handle non-finite values.
Results may differ from a plain program's by a relative error of at most 0.0037.
Values may be sent and summed in bfloat16 or wider, within the bound.
A program may use at most 128 MiB of HBM per device.

v0:
```python
import functools
import math
import jax
import jax.numpy as jnp
from jax import lax
from jax.sharding import Mesh
from jax.sharding import PartitionSpec as P

WALSH = 512
MIX = 14
FEATURES = 7168
BLK = ("blk_0", "blk_1")
TOK = ("tok_0", "tok_1", "tok_2")
TOK_BLK = ("tok_0", "tok_1", "tok_2", "blk_0", "blk_1")
EPS = 1e-06
DAMP = 0.01


def over_axes(value, axes):
    return functools.reduce(lax.psum, axes, value)


def laid_out(pieces, dim):
    pieces = jnp.moveaxis(pieces, 0, dim)
    dims = pieces.shape
    return pieces.reshape(*dims[:dim], dims[dim] * dims[dim + 1], *dims[dim + 2 :])


def from_everyone(value, axis):
    copies = jnp.broadcast_to(value, (lax.axis_size(axis), *value.shape))
    return lax.all_to_all(copies, axis, split_axis=0, concat_axis=0, tiled=True)


def gather_directly(value, axis, dim):
    return laid_out(from_everyone(value, axis), dim)


def over_copies(value, axis):
    everything = from_everyone(value, axis)
    return jnp.max(everything, axis=0)


def walsh_table(length):
    position = jnp.arange(length, dtype=jnp.int32)
    parity = jnp.zeros((length, length), jnp.int32)
    for bit_number in range(length.bit_length() - 1):
        parity = parity + (position[:, None] >> bit_number & 1) * (
            position[None, :] >> bit_number & 1
        )
    return (1 - 2 * (parity % 2)).astype(jnp.float32)


def cosine_table(length):
    rows_idx = jnp.arange(length, dtype=jnp.float32)[:, None]
    columns = jnp.arange(length, dtype=jnp.float32)[None, :]
    table = math.sqrt(2.0 / length) * jnp.cos(math.pi * (columns + 0.5) * rows_idx / length)
    return jnp.where(rows_idx == 0.0, table * math.sqrt(0.5), table)


def contract_tokens(left, right):
    return lax.dot_general(
        left, right, (((0,), (0,)), ((), ())), preferred_element_type=jnp.float32
    )


def per_device(activations, signs):
    tok_rows, block_width = activations.shape
    blocks = lax.axis_size(BLK)
    block_index = lax.axis_index(BLK)
    token_groups = lax.axis_size(TOK)
    token_index = lax.axis_index(TOK)
    local_walsh = WALSH // blocks
    signed = activations * signs.astype(jnp.bfloat16)[None, :]
    local_table = jnp.kron(walsh_table(local_walsh) / math.sqrt(local_walsh), cosine_table(MIX).T)
    partial_mix = jnp.dot(signed.astype(jnp.float32), local_table, precision=lax.Precision.HIGHEST)
    grouped = partial_mix.reshape(blocks, tok_rows // blocks, 1, block_width)
    cross_table = walsh_table(blocks) / math.sqrt(blocks)
    combined = jnp.einsum(
        "rs,xisf->xirf",
        cross_table,
        lax.all_to_all(grouped, BLK, split_axis=0, concat_axis=2, tiled=True),
        precision=lax.Precision.HIGHEST,
    )
    spread = lax.all_to_all(
        combined.astype(jnp.bfloat16), BLK, split_axis=2, concat_axis=0, tiled=True
    )
    rotated = spread.reshape(tok_rows, block_width)
    rotated_wide = rotated.astype(jnp.float32)
    trace_total = over_axes(jnp.sum(rotated_wide * rotated_wide), TOK_BLK)
    row_count = FEATURES // token_groups
    gathered = gather_directly(rotated, BLK, 1)
    gram_block = lax.psum_scatter(
        contract_tokens(gathered, rotated), TOK, scatter_dimension=0, tiled=True
    )
    global_rows = token_index * row_count + jnp.arange(row_count, dtype=jnp.int32)[:, None]
    global_columns = block_index * block_width + jnp.arange(block_width, dtype=jnp.int32)[None, :]
    on_diag = global_rows == global_columns
    local_peaks = jnp.max(jnp.where(on_diag, 0.0, jnp.abs(gram_block)), axis=0)
    column_peak = over_copies(local_peaks, TOK)
    diag_mean = trace_total / FEATURES + EPS
    hessian = gram_block / diag_mean + DAMP * on_diag.astype(jnp.float32)
    incoherence = column_peak / diag_mean
    largest_ratio = over_copies(jnp.max(incoherence), BLK)
    return (hessian, incoherence, largest_ratio)


def solution(mesh):
    split = Mesh(mesh.devices.reshape(4, 4, 2, 4, 2), ("tok_0", "tok_1", "tok_2", "blk_0", "blk_1"))
    return jax.shard_map(
        per_device,
        mesh=split,
        in_specs=(P(TOK, BLK), P(BLK)),
        out_specs=(P(TOK, BLK), P(BLK), P()),
        check_vma=False,
    )
```

profile of v0, /device:TPU:1, one launch (start us, length us, event | category | flops | bytes accessed | tf_op | source)
XLA Modules:
  0.0 367.2 jit_solution(6136312836264446147)
XLA Ops:
  7.2 0.1 multiply_select_fusion
  7.3 0.1 fusion.9
  7.5 13.5 %broadcast_multiply_fusion = f32[64,14,64,14]{3,2,1,0:T(8,128)} fusion(f32[14,14]{1,0:T(8,128)S(1)} %multiply_select_fusion, f32[64,64]{1,0:T(8,128)S(1)} %fusion.9), kind=kLoop, calls=%fused_computation | loop fusion | flops 802816 | bytes 3228432 | tf_op jit(solution)/shard_map/jit(kron)/mul | solution.py:74
  21.0 0.0 copy-start.1
  21.0 0.0 copy-start
  21.0 21.0 %reshape.408 = f32[896,896,1]{1,0,2:T(8,128)S(1)} reshape(f32[64,14,64,14]{3,2,1,0:T(8,128)} %broadcast_multiply_fusion) | data formatting | bytes 6422528 | tf_op jit(solution)/shard_map/jit(kron)/mul | solution.py:74
  42.0 0.0 copy-done.1
  42.0 0.0 copy-done
  42.0 2.2 convolution_bitcast_fusion
  44.2 11.6 %all-to-all-start = ((f32[8,16,1,896]{3,1,2,0:T(8,128)}), f32[8,16,1,896]{3,1,2,0:T(8,128)S(1)}, u32[]{:S(2)}, u32[]{:S(2)}) async-start(f32[8,16,1,896]{3,1,2,0:T(8,128)} %convolution_bitcast_fusion), calls=%async_computation | async-start | bytes 917504 | tf_op jit(solution)/shard_map/all_to_all | solution.py:81
  55.8 0.0 reduce-scatter.2.cloned.1.call-start
  55.9 12.6 %all-to-all-done = f32[8,16,1,896]{3,1,2,0:T(8,128)S(1)} async-done(((f32[8,16,1,896]{3,1,2,0:T(8,128)}), f32[8,16,1,896]{3,1,2,0:T(8,128)S(1)}, u32[]{:S(2)}, u32[]{:S(2)}) %all-to-all-start) | async-done | bytes 458784 | tf_op jit(solution)/shard_map/all_to_all | solution.py:81
  68.5 0.6 fusion
  69.1 12.3 %all_to_all.47 = bf16[1,16,8,896]{3,1,0,2:T(8,128)(2,1)S(1)} all-to-all(bf16[1,16,8,896]{3,1,0,2:T(8,128)(2,1)S(1)} %copy.19), channel_id=1, replica_groups=mesh['tok_0'=4,'tok_1'=4,'tok_2'=2,'blk_0'=4,'blk_1'=2] {'blk_0','blk_1'}, dimensions={2} | all-to-all | bytes 458752 | tf_op jit(solution)/shard_map/all_to_all | solution.py:84
  81.4 0.2 copy.20
  81.6 0.2 broadcast_in_dim.15
  81.8 24.9 %all_to_all.48 = bf16[8,128,896]{1,2,0:T(8,128)(2,1)S(1)} all-to-all(bf16[8,128,896]{1,2,0:T(8,128)(2,1)S(1)} %broadcast_in_dim.15), channel_id=1, replica_groups=mesh['tok_0'=4,'tok_1'=4,'tok_2'=2,'blk_0'=4,'blk_1'=2] {'blk_0','blk_1'}, dimensions={0} | all-to-all | bytes 3670016 | tf_op jit(solution)/shard_map/all_to_all | solution.py:31
  106.7 10.3 %fusion.35 = f32[7168,896]{1,0:T(8,128)} fusion(bf16[128,7168]{0,1:T(8,128)(2,1)S(1)} %bitcast.34, bf16[128,896]{1,0:T(8,128)(2,1)S(1)} %bitcast.36), kind=kOutput, calls=%fused_computation.62 | convolution fusion | flops 1644167168 | bytes 27754496 | tf_op jit(solution)/shard_map/dot_general | solution.py:61
  117.0 0.0 reduce-scatter.2.cloned.1.call-update
  117.0 0.7 multiply_reduce_fusion
  117.7 34.7 %psum.35 = f32[]{:T(128)} all-reduce(f32[]{:T(128)} %multiply_reduce_fusion), channel_id=1, replica_groups=mesh['tok_0'=4,'tok_1'=4,'tok_2'=2,'blk_0'=4,'blk_1'=2] {'tok_0'}, use_global_device_ids=true, to_apply=%region_2.3 | all-reduce | flops 1 | bytes 8 | tf_op jit(solution)/shard_map/psum | solution.py:20
  152.4 12.9 %psum.36 = f32[]{:T(128)} all-reduce(f32[]{:T(128)} %psum.35), channel_id=1, replica_groups=mesh['tok_0'=4,'tok_1'=4,'tok_2'=2,'blk_0'=4,'blk_1'=2] {'tok_1'}, use_global_device_ids=true, to_apply=%region_3.4 | all-reduce | flops 1 | bytes 8 | tf_op jit(solution)/shard_map/psum | solution.py:20
  165.4 3.8 %psum.37 = f32[]{:T(128)} all-reduce(f32[]{:T(128)} %psum.36), channel_id=1, replica_groups=mesh['tok_0'=4,'tok_1'=4,'tok_2'=2,'blk_0'=4,'blk_1'=2] {'tok_2'}, use_global_device_ids=true, to_apply=%region_4.5 | all-reduce | flops 1 | bytes 8 | tf_op jit(solution)/shard_map/psum | solution.py:20
  169.1 8.8 %psum.38 = f32[]{:T(128)} all-reduce(f32[]{:T(128)} %psum.37), channel_id=1, replica_groups=mesh['tok_0'=4,'tok_1'=4,'tok_2'=2,'blk_0'=4,'blk_1'=2] {'blk_0'}, use_global_device_ids=true, to_apply=%region_5.6 | all-reduce | flops 1 | bytes 8 | tf_op jit(solution)/shard_map/psum | solution.py:20
  178.0 8.7 %psum.39 = f32[]{:T(128)} all-reduce(f32[]{:T(128)} %psum.38), channel_id=1, replica_groups=mesh['tok_0'=4,'tok_1'=4,'tok_2'=2,'blk_0'=4,'blk_1'=2] {'blk_1'}, use_global_device_ids=true, to_apply=%region_6.7 | all-reduce | flops 1 | bytes 8 | tf_op jit(solution)/shard_map/psum | solution.py:20
  187.3 135.7 %reduce-scatter.2.cloned.1.call-done = f32[224,896]{1,0:T(8,128)} async-done(((f32[7168,896]{1,0:T(8,128)}), f32[224,896]{1,0:T(8,128)}) %reduce-scatter.2.cloned.1.call-update) | async-done | bytes 802832 | tf_op jit(solution)/shard_map/reduce_scatter | solution.py:92
  323.0 2.3 fusion.2
  325.2 0.1 broadcast_in_dim.16
  325.3 16.7 %all_to_all.49 = f32[32,1,896]{2,1,0:T(1,128)S(1)} all-to-all(f32[32,1,896]{2,1,0:T(1,128)S(1)} %broadcast_in_dim.16), channel_id=1, replica_groups=mesh['tok_0'=4,'tok_1'=4,'tok_2'=2,'blk_0'=4,'blk_1'=2] {'tok_0','tok_1'..., dimensions={0} | all-to-all | bytes 229376 | tf_op jit(solution)/shard_map/all_to_all | solution.py:31
  342.0 0.1 reduce_max.37
  342.1 1.2 fusion.34
  343.3 0.6 broadcast_in_dim.17
  343.9 15.8 %all_to_all.50 = f32[8,1,1]{2,1,0:T(1,128)S(1)} all-to-all(f32[8,1,1]{2,1,0:T(1,128)S(1)} %broadcast_in_dim.17), channel_id=1, replica_groups=mesh['tok_0'=4,'tok_1'=4,'tok_2'=2,'blk_0'=4,'blk_1'=2] {'blk_0','blk_1'}, dimensions={0} | all-to-all | bytes 64 | tf_op jit(solution)/shard_map/all_to_all | solution.py:31
  359.8 0.6 reduce_max.39
  (12 shorter events, 0.1 us)
Async XLA Ops:
  21.0 21.0 %copy-start.1 = (f32[896]{0:T(1024)S(1)}, f32[896]{0:T(1024)}, u32[]{:S(2)}) copy-start(f32[896]{0:T(1024)} %param.3) | copy-start | bytes 10756
  21.0 21.0 %copy-start = (bf16[128,896]{1,0:T(8,128)(2,1)S(1)}, bf16[128,896]{1,0:T(8,128)(2,1)}, u32[]{:S(2)}) copy-start(bf16[128,896]{1,0:T(8,128)(2,1)} %param.2) | copy-start | bytes 688132
  44.2 24.3 %all-to-all-start = ((f32[8,16,1,896]{3,1,2,0:T(8,128)}), f32[8,16,1,896]{3,1,2,0:T(8,128)S(1)}, u32[]{:S(2)}, u32[]{:S(2)}) async-start(f32[8,16,1,896]{3,1,2,0:T(8,128)} %convolution_bitcast_fusion), calls=%async_computation | async-start | bytes 917504 | tf_op jit(solution)/shard_map/all_to_all | solution.py:81
  55.8 267.1 %reduce-scatter.2.cloned.1.call-start = ((), (), s32[]{:S(2)}) async-start(), calls=%async_computation.6 | async-start | bytes 26492928 | tf_op jit(solution)/shard_map/reduce_scatter | solution.py:92
Sparse Core Ops, SparseCore 0:
  117.1 205.8 reduce-scatter.1
where the time goes:
time: 368 us; the launch traced here: 367 us
  waiting for transfers between devices  148 us (40%)
  blocking collectives  139 us (38%)
  local copies, waits for them, and re-layouts  22.1 us (6%)
  other arithmetic  18.7 us (5%)
  between operations  14.8 us (4%)
  matrix products  13.1 us (4%)
  starting transfers between devices  11.7 us (3%)
    reduce_scatter x1, waiting for transfers between devices, per_device(): lax.psum_scatter(contract_tokens(gathered, rotated), TOK, scatter_dimensi...  136 us
    psum x5, blocking collectives, over_axes(): return functools.reduce(lax.psum, axes, value)  69 us
    all_to_all x3, blocking collectives, from_everyone(): return lax.all_to_all(copies, axis, split_axis=0, concat_axis=0, tiled=True)  57.4 us
    mul x1, local copies, waits for them, and re-layouts, per_device(): jnp.kron(walsh_table(local_walsh) / math.sqrt(local_walsh), cosine_table(...  21 us
    mul x1, other arithmetic, per_device(): jnp.kron(walsh_table(local_walsh) / math.sqrt(local_walsh), cosine_table(...  13.5 us
    all_to_all x1, waiting for transfers between devices, per_device(): lax.all_to_all(grouped, BLK, split_axis=0, concat_axis=2, tiled=True)  12.6 us
    all_to_all x1, blocking collectives, per_device(): lax.all_to_all(combined.astype(jnp.bfloat16), BLK, split_axis=2, concat_a...  12.3 us
    all_to_all x1, starting transfers between devices, per_device(): lax.all_to_all(grouped, BLK, split_axis=0, concat_axis=2, tiled=True)  11.6 us
  transfers between devices with their start and end apart: 2, of which 2 were waited for; matrix products, arithmetic and copies ran while one was open for 0% of the time, Pallas kernels for 0%

commit v1 on v0

--- a/solution.py
+++ b/solution.py
@@ -14,6 +14,12 @@
 TOK_BLK = ("tok_0", "tok_1", "tok_2", "blk_0", "blk_1")
 EPS = 1e-06
 DAMP = 0.01
+
+
+def swap_blocks(x, name, split, join):
+    pieces = jnp.split(x, lax.axis_size(name), axis=split)
+    got = lax.all_to_all(jnp.stack(pieces), name, 0, 0)
+    return jnp.concatenate(got, axis=join)
 
 
 def over_axes(value, axes):
@@ -78,7 +84,7 @@
     combined = jnp.einsum(
         "rs,xisf->xirf",
         cross_table,
-        lax.all_to_all(grouped, BLK, split_axis=0, concat_axis=2, tiled=True),
+        swap_blocks(grouped, BLK, 0, 2),
         precision=lax.Precision.HIGHEST,
     )
     spread = lax.all_to_all(

time: 368 us -> 372 us (1.011)
  local copies, waits for them, and re-layouts: 22.1 us -> 27.1 us
    unnamed x4 -> x11, local copies, waits for them, and re-layouts: 0.01 us -> 4.39 us
where the time goes in v1:
time: 372 us; the launch traced here: 371 us
  waiting for transfers between devices  148 us (40%)
  blocking collectives  139 us (37%)
  local copies, waits for them, and re-layouts  27.1 us (7%)
  other arithmetic  18.7 us (5%)
  between operations  14.8 us (4%)
  matrix products  12.3 us (3%)
  starting transfers between devices  11.7 us (3%)
    reduce_scatter x1, waiting for transfers between devices, per_device(): lax.psum_scatter(contract_tokens(gathered, rotated), TOK, scatter_dimensi...  135 us
    psum x5, blocking collectives, over_axes(): return functools.reduce(lax.psum, axes, value)  68.9 us
    all_to_all x3, blocking collectives, from_everyone(): return lax.all_to_all(copies, axis, split_axis=0, concat_axis=0, tiled=True)  57.6 us
    mul x1, local copies, waits for them, and re-layouts, per_device(): jnp.kron(walsh_table(local_walsh) / math.sqrt(local_walsh), cosine_table(...  21 us
    mul x1, other arithmetic, per_device(): jnp.kron(walsh_table(local_walsh) / math.sqrt(local_walsh), cosine_table(...  13.5 us
    all_to_all x1, waiting for transfers between devices, swap_blocks(): got = lax.all_to_all(jnp.stack(pieces), name, 0, 0)  12.6 us
    all_to_all x1, blocking collectives, per_device(): lax.all_to_all(combined.astype(jnp.bfloat16), BLK, split_axis=2, concat_a...  12.3 us
    all_to_all x1, starting transfers between devices, swap_blocks(): got = lax.all_to_all(jnp.stack(pieces), name, 0, 0)  11.6 us
  transfers between devices with their start and end apart: 2, of which 2 were waited for; matrix products, arithmetic and copies ran while one was open for 0% of the time, Pallas kernels for 0%

profile of v1, /device:TPU:1, one launch (start us, length us, event | category | flops | bytes accessed | tf_op | source)
XLA Modules:
  0.0 371.4 jit_solution(14656806548572784562)
XLA Ops:
  7.2 0.1 multiply_select_fusion
  7.3 0.1 fusion.19
  7.5 13.5 %broadcast_multiply_fusion = f32[64,14,64,14]{3,2,1,0:T(8,128)} fusion(f32[14,14]{1,0:T(8,128)S(1)} %multiply_select_fusion, f32[64,64]{1,0:T(8,128)S(1)} %fusion.19), kind=kLoop, calls=%fused_computation | loop fusion | flops 802816 | bytes 3228432 | tf_op jit(solution)/shard_map/jit(kron)/mul | solution.py:80
  21.0 0.0 copy-start.1
  21.0 0.0 copy-start
  21.0 21.0 %mul.290 = f32[896,896]{1,0:T(8,128)S(1)} reshape(f32[64,14,64,14]{3,2,1,0:T(8,128)} %broadcast_multiply_fusion) | data formatting | bytes 6422528 | tf_op jit(solution)/shard_map/jit(kron)/mul | solution.py:80
  42.0 0.0 copy-done.1
  42.0 0.0 copy-done
  42.0 1.4 fusion.4
  43.4 0.6 fusion.14
  44.1 0.6 fusion.13
  44.7 0.6 fusion.12
  45.3 0.6 fusion.11
  45.9 0.6 fusion.10
  46.6 0.6 fusion.9
  47.2 0.6 fusion.8
  47.8 0.6 fusion.7
  48.4 11.6 %all-to-all-start = ((f32[8,1,16,1,896]{4,2,3,1,0:T(8,128)}), f32[8,1,16,1,896]{4,2,3,1,0:T(8,128)S(1)}, u32[]{:S(2)}, u32[]{:S(2)}) async-start(f32[8,1,16,1,896]{4,2,3,1,0:T(8,128)} %fusion.7), calls=%async_computation | async-start | bytes 917504 | tf_op jit(solution)/shard_map/all_to_all | solution.py:21
  60.1 0.0 reduce-scatter.2.cloned.1.call-start
  60.1 12.6 %all-to-all-done = f32[8,1,16,1,896]{4,2,3,1,0:T(8,128)S(1)} async-done(((f32[8,1,16,1,896]{4,2,3,1,0:T(8,128)}), f32[8,1,16,1,896]{4,2,3,1,0:T(8,128)S(1)}, u32[]{:S(2)}, u32[]{:S(2)}) %all-to-all-start) | async-done | bytes 458784 | tf_op jit(solution)/shard_map/all_to_all | solution.py:21
  72.7 0.6 fusion
  73.4 12.3 %all_to_all.37 = bf16[1,16,8,896]{3,1,0,2:T(8,128)(2,1)S(1)} all-to-all(bf16[1,16,8,896]{3,1,0,2:T(8,128)(2,1)S(1)} %copy.16), channel_id=1, replica_groups=mesh['tok_0'=4,'tok_1'=4,'tok_2'=2,'blk_0'=4,'blk_1'=2] {'blk_0','blk_1'}, dimensions={2} | all-to-all | bytes 458752 | tf_op jit(solution)/shard_map/all_to_all | solution.py:90
  85.7 0.2 copy.17
  85.8 0.2 broadcast_in_dim.15
  86.1 24.9 %all_to_all.38 = bf16[8,128,896]{1,2,0:T(8,128)(2,1)S(1)} all-to-all(bf16[8,128,896]{1,2,0:T(8,128)(2,1)S(1)} %broadcast_in_dim.15), channel_id=1, replica_groups=mesh['tok_0'=4,'tok_1'=4,'tok_2'=2,'blk_0'=4,'blk_1'=2] {'blk_0','blk_1'}, dimensions={0} | all-to-all | bytes 3670016 | tf_op jit(solution)/shard_map/all_to_all | solution.py:37
  111.0 10.3 %fusion.45 = f32[7168,896]{1,0:T(8,128)} fusion(bf16[128,7168]{0,1:T(8,128)(2,1)S(1)} %bitcast.56, bf16[128,896]{1,0:T(8,128)(2,1)S(1)} %bitcast.58), kind=kOutput, calls=%fused_computation.78 | convolution fusion | flops 1644167168 | bytes 27754496 | tf_op jit(solution)/shard_map/dot_general | solution.py:67
  121.2 0.0 reduce-scatter.2.cloned.1.call-update
  121.2 0.7 multiply_reduce_fusion
  122.0 34.7 %psum.35 = f32[]{:T(128)} all-reduce(f32[]{:T(128)} %multiply_reduce_fusion), channel_id=1, replica_groups=mesh['tok_0'=4,'tok_1'=4,'tok_2'=2,'blk_0'=4,'blk_1'=2] {'tok_0'}, use_global_device_ids=true, to_apply=%region_2.3 | all-reduce | flops 1 | bytes 8 | tf_op jit(solution)/shard_map/psum | solution.py:26
  156.7 12.9 %psum.36 = f32[]{:T(128)} all-reduce(f32[]{:T(128)} %psum.35), channel_id=1, replica_groups=mesh['tok_0'=4,'tok_1'=4,'tok_2'=2,'blk_0'=4,'blk_1'=2] {'tok_1'}, use_global_device_ids=true, to_apply=%region_3.4 | all-reduce | flops 1 | bytes 8 | tf_op jit(solution)/shard_map/psum | solution.py:26
  169.6 3.8 %psum.37 = f32[]{:T(128)} all-reduce(f32[]{:T(128)} %psum.36), channel_id=1, replica_groups=mesh['tok_0'=4,'tok_1'=4,'tok_2'=2,'blk_0'=4,'blk_1'=2] {'tok_2'}, use_global_device_ids=true, to_apply=%region_4.5 | all-reduce | flops 1 | bytes 8 | tf_op jit(solution)/shard_map/psum | solution.py:26
  173.4 8.8 %psum.38 = f32[]{:T(128)} all-reduce(f32[]{:T(128)} %psum.37), channel_id=1, replica_groups=mesh['tok_0'=4,'tok_1'=4,'tok_2'=2,'blk_0'=4,'blk_1'=2] {'blk_0'}, use_global_device_ids=true, to_apply=%region_5.6 | all-reduce | flops 1 | bytes 8 | tf_op jit(solution)/shard_map/psum | solution.py:26
  182.2 8.7 %psum.39 = f32[]{:T(128)} all-reduce(f32[]{:T(128)} %psum.38), channel_id=1, replica_groups=mesh['tok_0'=4,'tok_1'=4,'tok_2'=2,'blk_0'=4,'blk_1'=2] {'blk_1'}, use_global_device_ids=true, to_apply=%region_6.7 | all-reduce | flops 1 | bytes 8 | tf_op jit(solution)/shard_map/psum | solution.py:26
  191.6 135.4 %reduce-scatter.2.cloned.1.call-done = f32[224,896]{1,0:T(8,128)} async-done(((f32[7168,896]{1,0:T(8,128)}), f32[224,896]{1,0:T(8,128)}) %reduce-scatter.2.cloned.1.call-update) | async-done | bytes 802832 | tf_op jit(solution)/shard_map/reduce_scatter | solution.py:98
  327.0 2.3 fusion.2
  329.2 0.1 broadcast_in_dim.16
  329.3 16.7 %all_to_all.39 = f32[32,1,896]{2,1,0:T(1,128)S(1)} all-to-all(f32[32,1,896]{2,1,0:T(1,128)S(1)} %broadcast_in_dim.16), channel_id=1, replica_groups=mesh['tok_0'=4,'tok_1'=4,'tok_2'=2,'blk_0'=4,'blk_1'=2] {'tok_0','tok_1'..., dimensions={0} | all-to-all | bytes 229376 | tf_op jit(solution)/shard_map/all_to_all | solution.py:37
  346.0 0.1 reduce_max.37
  346.0 1.2 fusion.44
  347.2 0.6 broadcast_in_dim.17
  347.9 16.1 %all_to_all.40 = f32[8,1,1]{2,1,0:T(1,128)S(1)} all-to-all(f32[8,1,1]{2,1,0:T(1,128)S(1)} %broadcast_in_dim.17), channel_id=1, replica_groups=mesh['tok_0'=4,'tok_1'=4,'tok_2'=2,'blk_0'=4,'blk_1'=2] {'blk_0','blk_1'}, dimensions={0} | all-to-all | bytes 64 | tf_op jit(solution)/shard_map/all_to_all | solution.py:37
  364.0 0.6 reduce_max.39
  (11 shorter events, 0.1 us)
Async XLA Ops:
  21.0 21.0 %copy-start.1 = (f32[896]{0:T(1024)S(1)}, f32[896]{0:T(1024)}, u32[]{:S(2)}) copy-start(f32[896]{0:T(1024)} %param.3) | copy-start | bytes 10756
  21.0 21.0 %copy-start = (bf16[128,896]{1,0:T(8,128)(2,1)S(1)}, bf16[128,896]{1,0:T(8,128)(2,1)}, u32[]{:S(2)}) copy-start(bf16[128,896]{1,0:T(8,128)(2,1)} %param.2) | copy-start | bytes 688132
  48.4 24.3 %all-to-all-start = ((f32[8,1,16,1,896]{4,2,3,1,0:T(8,128)}), f32[8,1,16,1,896]{4,2,3,1,0:T(8,128)S(1)}, u32[]{:S(2)}, u32[]{:S(2)}) async-start(f32[8,1,16,1,896]{4,2,3,1,0:T(8,128)} %fusion.7), calls=%async_computation | async-start | bytes 917504 | tf_op jit(solution)/shard_map/all_to_all | solution.py:21
  60.1 266.9 %reduce-scatter.2.cloned.1.call-start = ((), (), s32[]{:S(2)}) async-start(), calls=%async_computation.6 | async-start | bytes 26492928 | tf_op jit(solution)/shard_map/reduce_scatter | solution.py:98
Sparse Core Ops, SparseCore 0:
  121.3 205.5 reduce-scatter.1
